TPU v7x, 8 devices: a whole 2x2x1 slice. The times are simulated.
8 devices in a mesh: dz: 2 (over z, y), dy: 2 (over x), dx: 2 (over core).
Axes of the slice: x: 2, y: 2, z: 1, core: 2. Of those that a mesh axis runs over, the one named last changes fastest.
Arguments:
- x_one: bfloat16 [16384, 2048], P(('dz', 'dy', 'dx'))
- g_one: bfloat16 [16384, 2048], P(('dz', 'dy', 'dx'))
- x_two: bfloat16 [16384, 2048], P(('dz', 'dy', 'dx'))
- g_two: bfloat16 [16384, 2048], P(('dz', 'dy', 'dx'))
- w_one: bfloat16 [2048, 5120], replicated
- w_two: bfloat16 [5120, 2048], replicated
- w_three: bfloat16 [2048, 5120], replicated
- w_four: bfloat16 [5120, 2048], replicated
Outputs:
- output 1: float32 [2048, 5120], replicated
- output 2: float32 [5120, 2048], replicated
- output 3: float32 [2048, 5120], replicated
- output 4: float32 [5120, 2048], replicated
- output 5: bfloat16 [16384, 2048], P(('dz', 'dy', 'dx'))
- output 6: bfloat16 [16384, 2048], P(('dz', 'dy', 'dx'))
All inputs are finite; a program needn't handle non-finite values.
Results may differ from a plain program's by a relative error of at most 0.00494.
Values are sent between devices in bfloat16 or wider.
A program may use at most 1.25 GiB of HBM per device.

v0:
```python
import jax
import jax.numpy as jnp
from jax import lax
from jax.sharding import PartitionSpec as P

GELU_C = 0.7978845608028654
GELU_A = 0.044715


def gelu_value(pre_act):
    pre_f = pre_act.astype(jnp.float32)
    return 0.5 * pre_f * (1.0 + jnp.tanh(GELU_C * (pre_f + GELU_A * pre_f * pre_f * pre_f)))


def gelu_slope(pre_act):
    pre_f = pre_act.astype(jnp.float32)
    tanh_val = jnp.tanh(GELU_C * (pre_f + GELU_A * pre_f * pre_f * pre_f))
    return 0.5 * (1.0 + tanh_val) + 0.5 * pre_f * (1.0 - tanh_val * tanh_val) * GELU_C * (1.0 + 3.0 * GELU_A * pre_f * pre_f)


def mat_tn(left_op, right_op):
    return lax.dot_general(left_op, right_op, (((0,), (0,)), ((), ())), preferred_element_type=jnp.float32)


def mat_nt(left_op, right_op):
    return lax.dot_general(left_op, right_op, (((1,), (1,)), ((), ())), preferred_element_type=jnp.float32)


def local_grads(x_rows, g_rows, w_one, w_two, w_three, w_four):
    pre_one = jnp.dot(x_rows, w_one, preferred_element_type=jnp.float32).astype(jnp.bfloat16)
    act_one = gelu_value(pre_one).astype(jnp.bfloat16)
    act_two = (jnp.dot(act_one, w_two, preferred_element_type=jnp.float32) + x_rows.astype(jnp.float32)).astype(jnp.bfloat16)
    pre_three = jnp.dot(act_two, w_three, preferred_element_type=jnp.float32).astype(jnp.bfloat16)
    act_three = gelu_value(pre_three).astype(jnp.bfloat16)
    grad_four = mat_tn(act_three, g_rows)
    dz_three = (mat_nt(g_rows, w_four) * gelu_slope(pre_three)).astype(jnp.bfloat16)
    grad_three = mat_tn(act_two, dz_three)
    dh_two = (mat_nt(dz_three, w_three) + g_rows.astype(jnp.float32)).astype(jnp.bfloat16)
    grad_two = mat_tn(act_one, dh_two)
    dz_one = (mat_nt(dh_two, w_two) * gelu_slope(pre_one)).astype(jnp.bfloat16)
    grad_one = mat_tn(x_rows, dz_one)
    dx_rows = (mat_nt(dz_one, w_one) + dh_two.astype(jnp.float32)).astype(jnp.bfloat16)
    return (grad_one, grad_two, grad_three, grad_four), dx_rows


def solution(mesh):
    dev_count = mesh.shape["dz"] * mesh.shape["dy"] * mesh.shape["dx"]
    row_spec = P(("dz", "dy", "dx"), None)
    rep_spec = P(None, None)

    def mean_over_devices(grad_sum):
        shard_sum = lax.psum_scatter(grad_sum, "dx", scatter_dimension=0, tiled=True)
        shard_sum = lax.psum_scatter(shard_sum, "dy", scatter_dimension=0, tiled=True)
        shard_sum = lax.psum_scatter(shard_sum, "dz", scatter_dimension=0, tiled=True)
        shard_mean = shard_sum / dev_count
        gathered = lax.all_gather(shard_mean, "dz", axis=0, tiled=True)
        gathered = lax.all_gather(gathered, "dy", axis=0, tiled=True)
        return lax.all_gather(gathered, "dx", axis=0, tiled=True)

    def per_device(x_one, g_one, x_two, g_two, w_one, w_two, w_three, w_four):
        grads_first, dx_first = local_grads(x_one, g_one, w_one, w_two, w_three, w_four)
        grads_second, dx_second = local_grads(x_two, g_two, w_one, w_two, w_three, w_four)
        mean_grads = [mean_over_devices(grad_a + grad_b) for grad_a, grad_b in zip(grads_first, grads_second)]
        return mean_grads[0], mean_grads[1], mean_grads[2], mean_grads[3], dx_first, dx_second

    return jax.shard_map(
        per_device,
        mesh=mesh,
        in_specs=(row_spec, row_spec, row_spec, row_spec, rep_spec, rep_spec, rep_spec, rep_spec),
        out_specs=(rep_spec, rep_spec, rep_spec, rep_spec, row_spec, row_spec),
        check_vma=False,
    )
```

profile of v0, /device:TPU:0, one launch (start us, length us, event | category | flops | bytes accessed | tf_op | source)
XLA Modules:
  0.0 4481.5 jit_solution(13341543034286677531)
XLA Ops:
  108.4 59.1 %add_convert_fusion.5 = bf16[2048,2048]{1,0:T(8,128)(2,1)} fusion(bf16[2048,2048]{1,0:T(8,128)(2,1)} %param.8, bf16[5120,2048]{1,0:T(8,128)(2,1)} %param.13, bf16[2048,5120]{1,0:T(8,128)(2,1)} %convolution_convert_fusion.3), kind=kOutput, calls=%fused_computation.94 | convolution fusion | flops 43067113472 | bytes 58720256 | tf_op jit(solution)/shard_map/dot_general | solution.py:32
  167.4 59.3 %add_convert_fusion.3 = bf16[2048,2048]{1,0:T(8,128)(2,1)} fusion(bf16[2048,2048]{1,0:T(8,128)(2,1)} %param.10, bf16[5120,2048]{1,0:T(8,128)(2,1)} %param.13, bf16[2048,5120]{1,0:T(8,128)(2,1)} %convolution_convert_fusion.1), kind=kOutput, calls=%fused_computation.92 | convolution fusion | flops 43067113472 | bytes 58720256 | tf_op jit(solution)/shard_map/dot_general | solution.py:32
  328.1 77.1 %fusion.24 = bf16[2048,5120]{1,0:T(8,128)(2,1)} fusion(bf16[2048,5120]{1,0:T(8,128)(2,1)} %convolution_convert_fusion.2, bf16[2048,2048]{1,0:T(8,128)(2,1)} %param.9, bf16[5120,2048]{1,0:T(8,128)(2,1)} %param.15), kind=kOutput, calls=%fused_computation.52 | convolution fusion | flops 43159388160 | bytes 71303168 | tf_op jit(solution)/shard_map/dot_general | solution.py:26
  458.1 77.2 %fusion.12 = bf16[2048,5120]{1,0:T(8,128)(2,1)} fusion(bf16[2048,5120]{1,0:T(8,128)(2,1)} %convolution_convert_fusion, bf16[2048,2048]{1,0:T(8,128)(2,1)} %param.11, bf16[5120,2048]{1,0:T(8,128)(2,1)} %param.15), kind=kOutput, calls=%fused_computation.40 | convolution fusion | flops 43159388160 | bytes 71303168 | tf_op jit(solution)/shard_map/dot_general | solution.py:26
  644.2 61.4 %fusion.63 = f32[5120,2048]{1,0:T(8,128)} fusion(bf16[2048,2048]{1,0:T(8,128)(2,1)} %add_convert_fusion.4, bf16[2048,5120]{1,0:T(8,128)(2,1)} %convolution_convert_fusion.3), kind=kOutput, calls=%fused_computation.107 | convolution fusion | flops 43054530560 | bytes 71303168 | tf_op jit(solution)/shard_map/dot_general | solution.py:22
  819.5 77.3 %fusion.31 = bf16[2048,5120]{1,0:T(8,128)(2,1)} fusion(bf16[2048,5120]{1,0:T(8,128)(2,1)} %convolution_convert_fusion.3, bf16[2048,2048]{1,0:T(8,128)(2,1)} %add_convert_fusion.4, bf16[5120,2048]{1,0:T(8,128)(2,1)} %param.13), kind=kOutput, calls=%fused_computation.59 | convolution fusion | flops 43159388160 | bytes 71303168 | tf_op jit(solution)/shard_map/dot_general | solution.py:26
  949.6 77.3 %fusion.19 = bf16[2048,5120]{1,0:T(8,128)(2,1)} fusion(bf16[2048,5120]{1,0:T(8,128)(2,1)} %convolution_convert_fusion.1, bf16[2048,2048]{1,0:T(8,128)(2,1)} %add_convert_fusion.2, bf16[5120,2048]{1,0:T(8,128)(2,1)} %param.13), kind=kOutput, calls=%fused_computation.47 | convolution fusion | flops 43159388160 | bytes 71303168 | tf_op jit(solution)/shard_map/dot_general | solution.py:26
  1080.5 61.0 %fusion.44 = f32[5120,2048]{1,0:T(8,128)} fusion(bf16[2048,2048]{1,0:T(8,128)(2,1)} %param.9, bf16[2048,5120]{1,0:T(8,128)(2,1)} %convolution_convert_fusion.2), kind=kOutput, calls=%fused_computation.76 | convolution fusion | flops 43054530560 | bytes 71303168 | tf_op jit(solution)/shard_map/dot_general | solution.py:22
  1247.8 234.6 %reduce-scatter.31.cloned.1.call-done = f32[512,5120]{0,1:T(8,128)} async-done(((f32[1024,5120]{0,1:T(8,128)}), f32[512,5120]{0,1:T(8,128)}) %reduce-scatter.31.cloned.1.call-update) | async-done | bytes 10485776 | tf_op jit(solution)/shard_map/reduce_scatter | solution.py:53
  1482.4 233.5 %reduce-scatter.25.cloned.1.call-done = f32[1280,2048]{1,0:T(8,128)} async-done(((f32[2560,2048]{1,0:T(8,128)}), f32[1280,2048]{1,0:T(8,128)}) %reduce-scatter.25.cloned.1.call-update) | async-done | bytes 10485776 | tf_op jit(solution)/shard_map/reduce_scatter | solution.py:53
  1716.0 233.6 %reduce-scatter.21.cloned.1.call-done = f32[512,5120]{0,1:T(8,128)} async-done(((f32[1024,5120]{0,1:T(8,128)}), f32[512,5120]{0,1:T(8,128)}) %reduce-scatter.21.cloned.1.call-update) | async-done | bytes 10485776 | tf_op jit(solution)/shard_map/reduce_scatter | solution.py:53
  1949.7 233.6 %reduce-scatter.35.cloned.1.call-done = f32[1280,2048]{1,0:T(8,128)} async-done(((f32[2560,2048]{1,0:T(8,128)}), f32[1280,2048]{1,0:T(8,128)}) %reduce-scatter.35.cloned.1.call-update) | async-done | bytes 10485776 | tf_op jit(solution)/shard_map/reduce_scatter | solution.py:53
  2183.4 121.3 %reduce-scatter.33.cloned.1.call-done = f32[256,5120]{0,1:T(8,128)} async-done(((f32[512,5120]{0,1:T(8,128)}), f32[256,5120]{0,1:T(8,128)}) %reduce-scatter.33.cloned.1.call-update) | async-done | bytes 5242896 | tf_op jit(solution)/shard_map/reduce_scatter | solution.py:54
  2310.0 115.9 %reduce-scatter.27.cloned.1.call-done = f32[640,2048]{1,0:T(8,128)} async-done(((f32[1280,2048]{1,0:T(8,128)}), f32[640,2048]{1,0:T(8,128)}) %reduce-scatter.27.cloned.1.call-update) | async-done | bytes 5242896 | tf_op jit(solution)/shard_map/reduce_scatter | solution.py:54
  2431.7 115.6 %reduce-scatter.23.cloned.1.call-done = f32[256,5120]{0,1:T(8,128)} async-done(((f32[512,5120]{0,1:T(8,128)}), f32[256,5120]{0,1:T(8,128)}) %reduce-scatter.23.cloned.1.call-update) | async-done | bytes 5242896 | tf_op jit(solution)/shard_map/reduce_scatter | solution.py:54
  2552.5 116.0 %reduce-scatter.37.cloned.1.call-done = f32[640,2048]{1,0:T(8,128)} async-done(((f32[1280,2048]{1,0:T(8,128)}), f32[640,2048]{1,0:T(8,128)}) %reduce-scatter.37.cloned.1.call-update) | async-done | bytes 5242896 | tf_op jit(solution)/shard_map/reduce_scatter | solution.py:54
  2674.3 123.9 %all-gather.25.cloned.1.call-done = f32[512,5120]{0,1:T(8,128)} async-done(((f32[256,5120]{0,1:T(8,128)}), f32[512,5120]{0,1:T(8,128)}) %all-gather.25.cloned.1.call-update) | async-done | bytes 10485776 | tf_op jit(solution)/shard_map/all_gather | solution.py:56
  2798.3 129.5 %all-gather.19.cloned.1.call-done = f32[1280,2048]{1,0:T(8,128)} async-done(((f32[640,2048]{1,0:T(8,128)}), f32[1280,2048]{1,0:T(8,128)}) %all-gather.19.cloned.1.call-update) | async-done | bytes 10485776 | tf_op jit(solution)/shard_map/all_gather | solution.py:56
  2927.8 129.5 %all-gather.13.cloned.1.call-done = f32[512,5120]{0,1:T(8,128)} async-done(((f32[256,5120]{0,1:T(8,128)}), f32[512,5120]{0,1:T(8,128)}) %all-gather.13.cloned.1.call-update) | async-done | bytes 10485776 | tf_op jit(solution)/shard_map/all_gather | solution.py:56
  3057.3 129.5 %all-gather.31.cloned.1.call-done = f32[1280,2048]{1,0:T(8,128)} async-done(((f32[640,2048]{1,0:T(8,128)}), f32[1280,2048]{1,0:T(8,128)}) %all-gather.31.cloned.1.call-update) | async-done | bytes 10485776 | tf_op jit(solution)/shard_map/all_gather | solution.py:56
  3186.9 246.3 %all-gather.27.cloned.1.call-done = f32[1024,5120]{0,1:T(8,128)} async-done(((f32[512,5120]{0,1:T(8,128)}), f32[1024,5120]{0,1:T(8,128)}) %all-gather.27.cloned.1.call-update) | async-done | bytes 20971536 | tf_op jit(solution)/shard_map/all_gather | solution.py:57
  3433.2 246.3 %all-gather.21.cloned.1.call-done = f32[2560,2048]{1,0:T(8,128)} async-done(((f32[1280,2048]{1,0:T(8,128)}), f32[2560,2048]{1,0:T(8,128)}) %all-gather.21.cloned.1.call-update) | async-done | bytes 20971536 | tf_op jit(solution)/shard_map/all_gather | solution.py:57
  3679.6 246.5 %all-gather.15.cloned.1.call-done = f32[1024,5120]{0,1:T(8,128)} async-done(((f32[512,5120]{0,1:T(8,128)}), f32[1024,5120]{0,1:T(8,128)}) %all-gather.15.cloned.1.call-update) | async-done | bytes 20971536 | tf_op jit(solution)/shard_map/all_gather | solution.py:57
  3926.2 246.3 %all-gather.33.cloned.1.call-done = f32[2560,2048]{1,0:T(8,128)} async-done(((f32[1280,2048]{1,0:T(8,128)}), f32[2560,2048]{1,0:T(8,128)}) %all-gather.33.cloned.1.call-update) | async-done | bytes 20971536 | tf_op jit(solution)/shard_map/all_gather | solution.py:57
  (82 shorter events, 1015.2 us)
Async XLA Ops:
  7.2 1193.3 %reduce-scatter.29.cloned.1.call-start = ((), (), s32[]{:S(2)}) async-start(), calls=%async_computation.23 | async-start | bytes 62914560 | tf_op jit(solution)/shard_map/reduce_scatter | solution.py:52
  589.1 611.9 %reduce-scatter.39.cloned.1.call-start = ((), (), s32[]{:S(2)}) async-start(), calls=%async_computation.34 | async-start | bytes 62914560
  819.4 382.2 %reduce-scatter.19.cloned.1.call-start = ((), (), s32[]{:S(2)}) async-start(), calls=%async_computation.12 | async-start | bytes 62914560 | tf_op jit(solution)/shard_map/reduce_scatter | solution.py:52
  1080.5 167.2 %reduce-scatter.41.cloned.1.call-start = ((), (), s32[]{:S(2)}) async-start(), calls=%async_computation.35 | async-start | bytes 62914560
  1200.4 282.0 %reduce-scatter.31.cloned.1.call-start = ((), (), s32[]{:S(2)}) async-start(), calls=%async_computation.24 | async-start | bytes 31457280 | tf_op jit(solution)/shard_map/reduce_scatter | solution.py:53
  1201.0 514.9 %reduce-scatter.25.cloned.1.call-start = ((), (), s32[]{:S(2)}) async-start(), calls=%async_computation.18 | async-start | bytes 31457280 | tf_op jit(solution)/shard_map/reduce_scatter | solution.py:53
  1201.6 748.1 %reduce-scatter.21.cloned.1.call-start = ((), (), s32[]{:S(2)}) async-start(), calls=%async_computation.13 | async-start | bytes 31457280 | tf_op jit(solution)/shard_map/reduce_scatter | solution.py:53
  1202.3 981.0 %reduce-scatter.35.cloned.1.call-start = ((), (), s32[]{:S(2)}) async-start(), calls=%async_computation.29 | async-start | bytes 31457280 | tf_op jit(solution)/shard_map/reduce_scatter | solution.py:53
  1247.7 1057.0 %reduce-scatter.33.cloned.1.call-start = ((), (), s32[]{:S(2)}) async-start(), calls=%async_computation.25 | async-start | bytes 15728640 | tf_op jit(solution)/shard_map/reduce_scatter | solution.py:54
  1482.4 943.5 %reduce-scatter.27.cloned.1.call-start = ((), (), s32[]{:S(2)}) async-start(), calls=%async_computation.19 | async-start | bytes 15728640 | tf_op jit(solution)/shard_map/reduce_scatter | solution.py:54
  1715.9 831.3 %reduce-scatter.23.cloned.1.call-start = ((), (), s32[]{:S(2)}) async-start(), calls=%async_computation.14 | async-start | bytes 15728640 | tf_op jit(solution)/shard_map/reduce_scatter | solution.py:54
  1949.7 718.8 %reduce-scatter.37.cloned.1.call-start = ((), (), s32[]{:S(2)}) async-start(), calls=%async_computation.30 | async-start | bytes 15728640 | tf_op jit(solution)/shard_map/reduce_scatter | solution.py:54
  2183.4 614.8 %all-gather.25.cloned.1.call-start = ((), (), s32[]{:S(2)}) async-start(), calls=%async_computation.26 | async-start | bytes 15728640 | tf_op jit(solution)/shard_map/all_gather | solution.py:56
  2309.9 617.8 %all-gather.19.cloned.1.call-start = ((), (), s32[]{:S(2)}) async-start(), calls=%async_computation.20 | async-start | bytes 15728640 | tf_op jit(solution)/shard_map/all_gather | solution.py:56
  2431.6 625.6 %all-gather.13.cloned.1.call-start = ((), (), s32[]{:S(2)}) async-start(), calls=%async_computation.15 | async-start | bytes 15728640 | tf_op jit(solution)/shard_map/all_gather | solution.py:56
  2552.5 634.3 %all-gather.31.cloned.1.call-start = ((), (), s32[]{:S(2)}) async-start(), calls=%async_computation.31 | async-start | bytes 15728640 | tf_op jit(solution)/shard_map/all_gather | solution.py:56
  2674.2 758.9 %all-gather.27.cloned.1.call-start = ((), (), s32[]{:S(2)}) async-start(), calls=%async_computation.27 | async-start | bytes 31457280 | tf_op jit(solution)/shard_map/all_gather | solution.py:57
  2798.2 881.4 %all-gather.21.cloned.1.call-start = ((), (), s32[]{:S(2)}) async-start(), calls=%async_computation.21 | async-start | bytes 31457280 | tf_op jit(solution)/shard_map/all_gather | solution.py:57
  2927.7 998.3 %all-gather.15.cloned.1.call-start = ((), (), s32[]{:S(2)}) async-start(), calls=%async_computation.16 | async-start | bytes 31457280 | tf_op jit(solution)/shard_map/all_gather | solution.py:57
  3057.3 1115.2 %all-gather.33.cloned.1.call-start = ((), (), s32[]{:S(2)}) async-start(), calls=%async_computation.32 | async-start | bytes 31457280 | tf_op jit(solution)/shard_map/all_gather | solution.py:57
  3186.8 1096.1 %all-gather.29.cloned.1.call-start = ((), (), s32[]{:S(2)}) async-start(), calls=%async_computation.28 | async-start | bytes 62914560 | tf_op jit(solution)/shard_map/all_gather | solution.py:58
  3433.2 888.5 %all-gather.23.cloned.1.call-start = ((), (), s32[]{:S(2)}) async-start(), calls=%async_computation.22 | async-start | bytes 62914560 | tf_op jit(solution)/shard_map/all_gather | solution.py:58
  3679.6 675.8 %all-gather.17.cloned.1.call-start = ((), (), s32[]{:S(2)}) async-start(), calls=%async_computation.17 | async-start | bytes 62914560 | tf_op jit(solution)/shard_map/all_gather | solution.py:58
  3926.1 490.5 %all-gather.35.cloned.1.call-start = ((), (), s32[]{:S(2)}) async-start(), calls=%async_computation.33 | async-start | bytes 62914560 | tf_op jit(solution)/shard_map/all_gather | solution.py:58
  (2 other events, 103.0 us)
Sparse Core Ops, SparseCore 0:
  589.2 47.1 reduce-scatter.28
  819.5 47.1 reduce-scatter.38
  1080.6 47.1 reduce-scatter.18
  1200.5 47.1 reduce-scatter.40
  1249.8 232.4 reduce-scatter.30
  1484.5 231.3 reduce-scatter.24
  1718.2 231.4 reduce-scatter.20
  1951.9 231.4 reduce-scatter.34
  2185.6 119.0 reduce-scatter.32
  2306.8 119.0 reduce-scatter.26
  2428.2 119.0 reduce-scatter.22
  2549.4 119.0 reduce-scatter.36
  2670.6 127.5 all-gather.24
  2800.1 127.5 all-gather.18
  2929.7 127.5 all-gather.12
  3059.2 127.5 all-gather.30
  3188.2 244.9 all-gather.26
  3434.5 244.9 all-gather.20
  3681.1 244.9 all-gather.14
  3927.5 244.9 all-gather.32
  4174.0 58.6 all-gather.28
  4234.2 59.7 all-gather.22
  4295.5 59.7 all-gather.16
  4356.7 59.7 all-gather.34
where the time goes:
time: 4490 us; the launch traced here: 4480 us
  waiting for transfers between devices  3010 us (67%)
  matrix products  1300 us (29%)
  local copies, waits for them, and re-layouts  135 us (3%)
    all_gather x4, waiting for transfers between devices, mean_over_devices(): gathered = lax.all_gather(gathered, 'dy', axis=0, tiled=True)  985 us
    reduce_scatter x4, waiting for transfers between devices, mean_over_devices(): lax.psum_scatter(shard_sum, 'dy', scatter_dimension=0, tiled=True)  935 us
    dot_general x8, matrix products, mat_nt(): lax.dot_general(left_op, right_op, (((1,), (1,)), ((), ())), preferred_el...  529 us
    all_gather x4, waiting for transfers between devices, mean_over_devices(): gathered = lax.all_gather(shard_mean, 'dz', axis=0, tiled=True)  512 us
    reduce_scatter x4, waiting for transfers between devices, mean_over_devices(): lax.psum_scatter(shard_sum, 'dz', scatter_dimension=0, tiled=True)  469 us
    dot_general x8, matrix products, mat_tn(): lax.dot_general(left_op, right_op, (((0,), (0,)), ((), ())), preferred_el...  453 us
    unnamed x8, local copies, waits for them, and re-layouts  135 us
    dot_general x2, matrix products, local_grads(): jnp.dot(act_one, w_two, preferred_element_type=jnp.float32)  118 us
  transfers between devices with their start and end apart: 24, of which 19 were waited for; matrix products, arithmetic and copies ran while one was open for 18% of the time, Pallas kernels for 0%

commit v1 on v0

v1 whole, which is shorter than its diff:
```python
import jax
import jax.numpy as jnp
from jax import lax
from jax.experimental import pallas as pl
from jax.experimental.pallas import tpu as pltpu
from jax.sharding import PartitionSpec as P

GELU_C = 0.7978845608028654
GELU_A = 0.044715
SWAP = [(0, 1), (1, 0)]
FF_TILE = 512


STEPS = (
    ("F1", 0), ("F1", 1), ("F2", 0), ("F2", 1),
    ("F3", 0, 0), ("F3", 0, 1), ("S", 4, 0), ("F3", 1, 0), ("C", 4, 0), ("F3", 1, 1), ("S", 4, 1), ("K", 4, 0), ("C", 4, 1), ("K", 4, 1),
    ("U", 4, 0), ("B3", 0, 0), ("B3", 0, 1), ("S", 3, 0), ("G", 4, 0), ("U", 4, 1), ("B3", 1, 0), ("C", 3, 0), ("B3", 1, 1), ("S", 3, 1), ("G", 4, 1),
    ("K", 3, 0), ("C", 3, 1), ("K", 3, 1), ("B2", 0), ("U", 3, 0), ("B2", 1), ("S", 2, 0), ("S", 2, 1), ("U", 3, 1), ("C", 2, 0), ("B1", 0, 0),
    ("C", 2, 1), ("B1", 0, 1), ("G", 3, 0), ("S", 1, 0), ("B1", 1, 0), ("C", 1, 0), ("B1", 1, 1), ("G", 3, 1), ("S", 1, 1), ("K", 2, 0), ("C", 1, 1), ("U", 2, 0),
    ("K", 2, 1), ("K", 1, 0), ("U", 2, 1), ("K", 1, 1), ("BX", 0), ("G", 2, 0), ("BX", 1), ("R", 4), ("G", 2, 1), ("U", 1, 0), ("R", 3),
    ("U", 1, 1), ("G", 1, 0), ("G", 1, 1), ("R", 2), ("R", 1),
)


def gelu_value(pre_act):
    pre_f = pre_act.astype(jnp.float32)
    return 0.5 * pre_f * (1.0 + jnp.tanh(GELU_C * (pre_f + GELU_A * pre_f * pre_f * pre_f)))


def gelu_slope(pre_act):
    pre_f = pre_act.astype(jnp.float32)
    square = pre_f * pre_f
    tanh_val = jnp.tanh(pre_f * (GELU_C + (GELU_C * GELU_A) * square))
    return (0.5 + 0.5 * tanh_val) * (1.0 + (pre_f * (1.0 - tanh_val)) * (GELU_C + (3.0 * GELU_C * GELU_A) * square))


def mat_nn(left_op, right_op):
    return jnp.dot(left_op, right_op, preferred_element_type=jnp.float32)


def mat_nt(left_op, right_op):
    return lax.dot_general(left_op, right_op, (((1,), (1,)), ((), ())), preferred_element_type=jnp.float32)


def mat_tn(left_op, right_op):
    return lax.dot_general(left_op, right_op, (((0,), (0,)), ((), ())), preferred_element_type=jnp.float32)


def grad_blocks(dim_ops, ff_ops, blocks, offset, wide_first, block):
    count = len(dim_ops)
    rows = dim_ops[0].shape[0]
    half = 10 * block
    tiles = half // FF_TILE

    def body(blocks_ref, *refs):
        dim_refs, ff_refs, out_refs = refs[: 4 * count], refs[4 * count : 5 * count], refs[5 * count :]
        for i in range(4):
            value = None
            for m in range(count):
                dim_val, ff_val = dim_refs[4 * m + i][...], ff_refs[m][...]
                term = mat_tn(ff_val, dim_val) if wide_first else mat_tn(dim_val, ff_val)
                value = term if value is None else value + term
            lo = (i % 2) * block
            if wide_first:
                out_refs[i // 2][:, lo : lo + block] = value
            else:
                out_refs[i // 2][lo : lo + block, :] = value

    def dim_spec(i):
        return pl.BlockSpec((rows, block), lambda j, b: (0, b[i]))

    if wide_first:
        out_shape = jax.ShapeDtypeStruct((half, 2 * block), jnp.float32)
        out_spec = pl.BlockSpec((FF_TILE, 2 * block), lambda j, b: (j, 0))
    else:
        out_shape = jax.ShapeDtypeStruct((2 * block, half), jnp.float32)
        out_spec = pl.BlockSpec((2 * block, FF_TILE), lambda j, b: (0, j))
    return pl.pallas_call(
        body,
        grid_spec=pltpu.PrefetchScalarGridSpec(
            num_scalar_prefetch=1,
            grid=(tiles,),
            in_specs=[dim_spec(i) for _ in range(count) for i in range(4)]
            + [pl.BlockSpec((rows, FF_TILE), lambda j, b: (0, offset * tiles + j)) for _ in range(count)],
            out_specs=[out_spec, out_spec],
        ),
        out_shape=[out_shape, out_shape],
        compiler_params=pltpu.CompilerParams(vmem_limit_bytes=62 * 1024 * 1024, dimension_semantics=("arbitrary",)),
        cost_estimate=pl.CostEstimate(flops=8 * count * rows * block * half, bytes_accessed=2 * count * rows * (half + 4 * block) + 16 * block * half, transcendentals=0),
    )(blocks, *[op for op in dim_ops for _ in range(4)], *ff_ops)


def solution(mesh):
    dev_count = mesh.shape["dz"] * mesh.shape["dy"] * mesh.shape["dx"]
    row_spec = P(("dz", "dy", "dx"), None)
    rep_spec = P(None, None)

    def per_device(x_one, g_one, x_two, g_two, w_one, w_two, w_three, w_four):
        dim, ff = w_one.shape
        block = dim // dev_count
        half_ff = ff // 2
        idx_z, idx_y, idx_c = lax.axis_index("dz"), lax.axis_index("dy"), lax.axis_index("dx")
        anchor = [x_one]

        def at(*vals):
            out = lax.optimization_barrier((*vals, anchor[0]))[:-1]
            return out if len(out) > 1 else out[0]

        def mark(val):
            anchor[0] = val
            return val

        def block_ids(color, send):
            ids = []
            for core in (1 - idx_c, idx_c):
                if color == 0:
                    col = 1 - idx_y if send else idx_y
                    ids += [4 * core + 2 * (1 - idx_z) + col, 4 * core + 2 * idx_z + col]
                else:
                    row = 1 - idx_z if send else idx_z
                    ids += [4 * core + 2 * row + 1 - idx_y, 4 * core + 2 * row + idx_y]
            return jnp.stack(ids).astype(jnp.int32)

        ids = {(color, send): block_ids(color, send) for color in (0, 1) for send in (False, True)}

        class Grad:
            def __init__(self, dim_ops, wide_first):
                self.dim_ops, self.wide_first = dim_ops, wide_first
                self.axis = 1 if wide_first else 0
                self.ff_ops, self.send, self.keep, self.chip, self.rows, self.full = {}, {}, {}, {}, {}, {}

            def link(self, color, second):
                return "dz" if (color == 0) == second else "dy"

            def product(self, color, send):
                ops = self.ff_ops[color]
                offset = color if ops[0].shape[1] > half_ff else 0
                part, own = grad_blocks([self.dim_ops[m] for m in (0, 1)], [at(ops[0]), ops[1]], ids[color, send], offset, self.wide_first, block)
                mark(own)
                got = lax.ppermute(part, "dx", SWAP)
                (self.send if send else self.keep)[color] = (own, got)

            def add_chip(self, color):
                own, got = self.send[color]
                chip = mark(at(own) + got)
                self.chip[color] = lax.ppermute(chip, self.link(color, False), SWAP)

            def add_rows(self, color):
                own, got = self.keep[color]
                total = mark(at(own) + got + self.chip[color])
                out, kept = jnp.split(total, 2, axis=self.axis)
                self.rows[color] = (kept, lax.ppermute(out, self.link(color, True), SWAP))

            def gather(self, color):
                kept, got = self.rows[color]
                shard = mark(at(kept) + got)
                self.full[color] = lax.all_gather(shard, ("dx", "dz", "dy"), axis=self.axis, tiled=True)

            def result(self):
                parts = [at(self.full[0]), self.full[1]]
                return mark(jnp.concatenate(parts, axis=1 - self.axis) / dev_count)

        def half(mat, color, axis):
            return lax.slice_in_dim(mat, color * half_ff, (color + 1) * half_ff, axis=axis)

        x_rows, g_rows = [x_one, x_two], [g_one, g_two]
        pre_one, act_one, act_two, dh_two, dx_rows = {}, {}, {}, {}, {}
        pre_three, act_three, dz_three, dz_one = ({0: {}, 1: {}} for _ in range(4))

        def forward_one(m):
            pre = mat_nn(x_rows[m], at(w_one)).astype(jnp.bfloat16)
            pre_one[m], act_one[m] = lax.optimization_barrier((pre, gelu_value(pre).astype(jnp.bfloat16)))
            mark(act_one[m])

        def forward_two(m):
            act_two[m] = mark((mat_nn(act_one[m], at(w_two)) + x_rows[m].astype(jnp.float32)).astype(jnp.bfloat16))

        def forward_three(color, m):
            pre = mat_nn(act_two[m], half(at(w_three), color, 1)).astype(jnp.bfloat16)
            pre_three[color][m], act_three[color][m] = lax.optimization_barrier((pre, gelu_value(pre).astype(jnp.bfloat16)))
            mark(act_three[color][m])

        def back_three(color, m):
            dz = mat_nt(g_rows[m], half(at(w_four), color, 0)) * gelu_slope(pre_three[color][m])
            dz_three[color][m] = mark(dz.astype(jnp.bfloat16))

        def back_two(m):
            weight = at(w_three)
            terms = mat_nt(dz_three[0][m], half(weight, 0, 1)) + mat_nt(dz_three[1][m], half(weight, 1, 1))
            dh_two[m] = mark((terms + g_rows[m].astype(jnp.float32)).astype(jnp.bfloat16))

        def back_one(color, m):
            dz = mat_nt(dh_two[m], half(at(w_two), color, 0)) * gelu_slope(half(pre_one[m], color, 1))
            dz_one[color][m] = mark(dz.astype(jnp.bfloat16))

        def back_x(m):
            weight = at(w_one)
            terms = mat_nt(dz_one[0][m], half(weight, 0, 1)) + mat_nt(dz_one[1][m], half(weight, 1, 1))
            dx_rows[m] = mark((terms + dh_two[m].astype(jnp.float32)).astype(jnp.bfloat16))

        four = Grad(g_rows, True)
        three = Grad(act_two, False)
        two = Grad(dh_two, True)
        one = Grad(x_rows, False)
        four.ff_ops, three.ff_ops, one.ff_ops = act_three, dz_three, dz_one
        two.ff_ops = {0: act_one, 1: act_one}
        grads = {4: four, 3: three, 2: two, 1: one}
        compute = {"F1": forward_one, "F2": forward_two, "F3": forward_three, "B3": back_three, "B2": back_two, "B1": back_one, "BX": back_x}
        results = {}
        for name, *args in STEPS:
            if name in compute:
                compute[name](*args)
            elif name in "SK":
                grads[args[0]].product(args[1], name == "S")
            elif name == "C":
                grads[args[0]].add_chip(args[1])
            elif name == "U":
                grads[args[0]].add_rows(args[1])
            elif name == "G":
                grads[args[0]].gather(args[1])
            else:
                results[args[0]] = grads[args[0]].result()
        return results[1], results[2], results[3], results[4], dx_rows[0], dx_rows[1]

    return jax.shard_map(
        per_device,
        mesh=mesh,
        in_specs=(row_spec, row_spec, row_spec, row_spec, rep_spec, rep_spec, rep_spec, rep_spec),
        out_specs=(rep_spec, rep_spec, rep_spec, rep_spec, row_spec, row_spec),
        check_vma=False,
    )
```

time: 4490 us -> 2690 us (0.60)
  waiting for transfers between devices: 3010 us -> 965 us
  Pallas kernels: 0 us -> 475 us
  matrix products: 1300 us -> 903 us
  other arithmetic: 21.7 us -> 267 us
  local copies, waits for them, and re-layouts: 135 us -> 30.5 us
    all_gather x12 -> x8, waiting for transfers between devices: 1550 us -> 111 us  [gather(): lax.all_gather(shard, ('dx', 'dz', 'dy'), axis=self.axis, tiled=True)]
    reduce_scatter x10 -> x0, waiting for transfers between devices: 1400 us -> none  [the longest x4 935 us: mean_over_devices(): lax.psum_scatter(shard_sum, 'dy', scatter_dimension=0, tiled=True)]
    ppermute x0 -> x32, waiting for transfers between devices: none -> 853 us  [the longest x8 652 us: add_chip(): self.chip[color] = lax.ppermute(chip, self.link(color, False), SWAP)]
    pallas_call x0 -> x16, Pallas kernels: none -> 475 us  [grad_blocks(): pl.pallas_call(body, grid_spec=pltpu.PrefetchScalarGridSpec(num_scalar_pr...]
    dot_general x14 -> x8, matrix products: 774 us -> 358 us  [mat_nn(): return jnp.dot(left_op, right_op, preferred_element_type=jnp.float32)]
    add x0 -> x24, other arithmetic: none -> 148 us  [the longest x8 67.6 us: add_rows(): total = mark(at(own) + got + self.chip[color])]
    unnamed x8 -> x54, local copies, waits for them, and re-layouts: 135 us -> 0.11 us
    div x4, other arithmetic: 21.7 us -> 117 us  [result(): return mark(jnp.concatenate(parts, axis=1 - self.axis) / dev_count)]
  transfers between devices with their start and end apart: 24 -> 40, of which waited for: 19 -> 12; matrix products, arithmetic and copies ran while one was open for 18% -> 29% of each run, Pallas kernels for 0% -> 15%
where the time goes in v1:
time: 2690 us; the launch traced here: 2680 us
  waiting for transfers between devices  965 us (36%)
  matrix products  903 us (34%)
  Pallas kernels  475 us (18%)
  other arithmetic  267 us (10%)
  local copies, waits for them, and re-layouts  30.5 us (1%)
    ppermute x8, waiting for transfers between devices, add_chip(): self.chip[color] = lax.ppermute(chip, self.link(color, False), SWAP)  652 us
    dot_general x16, matrix products, mat_nt(): lax.dot_general(left_op, right_op, (((1,), (1,)), ((), ())), preferred_el...  545 us
    pallas_call x16, Pallas kernels, grad_blocks(): pl.pallas_call(body, grid_spec=pltpu.PrefetchScalarGridSpec(num_scalar_pr...  475 us
    dot_general x8, matrix products, mat_nn(): return jnp.dot(left_op, right_op, preferred_element_type=jnp.float32)  358 us
    ppermute x8, waiting for transfers between devices, add_rows(): self.rows[color] = (kept, lax.ppermute(out, self.link(color, True), SWAP))  193 us
    div x4, other arithmetic, result(): return mark(jnp.concatenate(parts, axis=1 - self.axis) / dev_count)  117 us
    all_gather x8, waiting for transfers between devices, gather(): lax.all_gather(shard, ('dx', 'dz', 'dy'), axis=self.axis, tiled=True)  111 us
    add x8, other arithmetic, add_rows(): total = mark(at(own) + got + self.chip[color])  67.6 us
  transfers between devices with their start and end apart: 40, of which 12 were waited for; matrix products, arithmetic and copies ran while one was open for 29% of the time, Pallas kernels for 15%

profile of v1, /device:TPU:0, one launch (start us, length us, event | category | flops | bytes accessed | tf_op | source)
XLA Modules:
  0.0 2681.2 jit_solution(15873206718076901500)
XLA Ops:
  7.2 61.9 %fusion.1 = (bf16[2048,5120]{1,0:T(8,128)(2,1)}, bf16[2048,5120]{1,0:T(8,128)(2,1)}) fusion(bf16[2048,2048]{1,0:T(8,128)(2,1)} %refs_3_.15, bf16[2048,5120]{1,0:T(8,128)(2,1)} %param.12), kind=kOutput, calls=%fused_computation.11 | convolution fusion | flops 43065016320 | bytes 71303168 | tf_op jit(solution)/shard_map/dot_general | solution.py:38
  69.1 60.2 %fusion.6 = (bf16[2048,5120]{1,0:T(8,128)(2,1)}, bf16[2048,5120]{1,0:T(8,128)(2,1)}) fusion(bf16[2048,2048]{1,0:T(8,128)(2,1)S(1)} %copy-done, bf16[2048,5120]{1,0:T(8,128)(2,1)} %param.12), kind=kOutput, calls=%fused_computation.16 | convolution fusion | flops 43065016320 | bytes 71303168 | tf_op jit(solution)/shard_map/dot_general | solution.py:38
  129.3 53.0 %add_convert_fusion.5.refs_0_.refs_1_.refs_2_.refs_3_ = bf16[2048,2048]{1,0:T(8,128)(2,1)} fusion(bf16[2048,2048]{1,0:T(8,128)(2,1)} %refs_3_.15, bf16[2048,5120]{1,0:T(8,128)(2,1)} %get-tuple-element.200.refs_8_, bf16[5120,2048]{1,0:T(8,128)(2,1)} %param.13), kind=kOutput, calls=%fused_computation.175 | convolution fusion | flops 42962255872 | bytes 58720256 | tf_op jit(solution)/shard_map/dot_general | solution.py:38
  182.2 53.2 %add_convert_fusion.4.refs_4_.refs_5_.refs_6_.refs_7_ = bf16[2048,2048]{1,0:T(8,128)(2,1)} fusion(bf16[2048,2048]{1,0:T(8,128)(2,1)} %refs_7_.15, bf16[2048,5120]{1,0:T(8,128)(2,1)} %get-tuple-element.117.refs_9_, bf16[5120,2048]{1,0:T(8,128)(2,1)} %param.13), kind=kOutput, calls=%fused_computation.174 | convolution fusion | flops 42962255872 | bytes 58720256 | tf_op jit(solution)/shard_map/dot_general | solution.py:38
  235.4 32.8 %fusion.91 = (bf16[2048,2560]{1,0:T(8,128)(2,1)}, bf16[2048,2560]{1,0:T(8,128)(2,1)}) fusion(bf16[2048,2048]{1,0:T(8,128)(2,1)} %add_convert_fusion.5.refs_0_.refs_1_.refs_2_.refs_3_, bf16[2048,5120]{1,0:T(8,128)(2,1)} %param.14), kind=kOutput, calls=%fused_computation.149 | convolution fusion | flops 21532508160 | bytes 39845888 | tf_op jit(solution)/shard_map/dot_general | solution.py:38
  331.0 32.8 %fusion.101 = (bf16[2048,2560]{1,0:T(8,128)(2,1)}, bf16[2048,2560]{1,0:T(8,128)(2,1)}) fusion(bf16[2048,2048]{1,0:T(8,128)(2,1)} %add_convert_fusion.5.refs_0_.refs_1_.refs_2_.refs_3_, bf16[2048,5120]{1,0:T(8,128)(2,1)} %param.14), kind=kOutput, calls=%fused_computation.159 | convolution fusion | flops 21532508160 | bytes 39845888 | tf_op jit(solution)/shard_map/dot_general | solution.py:38
  372.2 32.6 %fusion.106 = (bf16[2048,2560]{1,0:T(8,128)(2,1)}, bf16[2048,2560]{1,0:T(8,128)(2,1)}) fusion(bf16[2048,2048]{1,0:T(8,128)(2,1)} %add_convert_fusion.4.refs_4_.refs_5_.refs_6_.refs_7_, bf16[2048,5120]{1,0:T(8,128)(2,1)} %param.14), kind=kOutput, calls=%fused_computation.164 | convolution fusion | flops 21532508160 | bytes 39845888 | tf_op jit(solution)/shard_map/dot_general | solution.py:38
  505.4 75.9 %collective-permute-done.3 = f32[2560,512]{1,0:T(8,128)} collective-permute-done((f32[2560,512]{1,0:T(8,128)}, f32[2560,512]{1,0:T(8,128)}, u32[]{:S(2)}, u32[]{:S(2)}) %collective-permute-start.3) | collective-permute-done | bytes 5242912 | tf_op jit(solution)/shard_map/ppermute | solution.py:146
  591.5 36.1 %fusion.81.refs_8_ = bf16[2048,2560]{1,0:T(8,128)(2,1)} fusion(bf16[2048,2560]{1,0:T(8,128)(2,1)} %get-tuple-element.143, bf16[2048,2048]{1,0:T(8,128)(2,1)S(1)} %bitcast.53, bf16[5120,2048]{1,0:T(8,128)(2,1)} %param.15), kind=kOutput, calls=%fused_computation.139 | convolution fusion | flops 21558722560 | bytes 39845888 | tf_op jit(solution)/shard_map/dot_general | solution.py:42
  629.4 37.0 %fusion.74.refs_9_ = bf16[2048,2560]{1,0:T(8,128)(2,1)} fusion(bf16[2048,2560]{1,0:T(8,128)(2,1)} %get-tuple-element.145, bf16[2048,2048]{1,0:T(8,128)(2,1)} %refs_7_.11, bf16[5120,2048]{1,0:T(8,128)(2,1)} %param.15), kind=kOutput, calls=%fused_computation.132 | convolution fusion | flops 21558722560 | bytes 39845888 | tf_op jit(solution)/shard_map/dot_general | solution.py:42
  709.4 191.2 %collective-permute-done.6 = f32[2560,512]{1,0:T(8,128)} collective-permute-done((f32[2560,512]{1,0:T(8,128)}, f32[2560,512]{1,0:T(8,128)}, u32[]{:S(2)}, u32[]{:S(2)}) %collective-permute-start.6) | collective-permute-done | bytes 5242912 | tf_op jit(solution)/shard_map/ppermute | solution.py:146
  909.1 36.9 %fusion.67.refs_8_ = bf16[2048,2560]{1,0:T(8,128)(2,1)} fusion(bf16[2048,2560]{1,0:T(8,128)(2,1)} %get-tuple-element.152, bf16[2048,2048]{1,0:T(8,128)(2,1)} %refs_3_.11, bf16[5120,2048]{1,0:T(8,128)(2,1)} %param.15), kind=kOutput, calls=%fused_computation.125 | convolution fusion | flops 21558722560 | bytes 39845888 | tf_op jit(solution)/shard_map/dot_general | solution.py:42
  951.7 36.2 %fusion.60.refs_9_ = bf16[2048,2560]{1,0:T(8,128)(2,1)} fusion(bf16[2048,2560]{1,0:T(8,128)(2,1)} %get-tuple-element.156, bf16[2048,2048]{1,0:T(8,128)(2,1)S(1)} %bitcast.55, bf16[5120,2048]{1,0:T(8,128)(2,1)} %param.15), kind=kOutput, calls=%fused_computation.118 | convolution fusion | flops 21558722560 | bytes 39845888 | tf_op jit(solution)/shard_map/dot_general | solution.py:42
  1022.2 57.7 %collective-permute-done.8 = f32[2560,256]{1,0:T(8,128)S(1)} collective-permute-done((f32[2560,256]{1,0:T(8,128)S(1)}, f32[2560,256]{1,0:T(8,128)S(1)}, u32[]{:S(2)}, u32[]{:S(2)}) %collective-permute-start.8) | collective-permute-done | bytes 2621472 | tf_op jit(solution)/shard_map/ppermute | solution.py:152
  1179.3 35.3 %add_convert_fusion.3.refs_0_.refs_1_.refs_2_.refs_3_ = bf16[2048,2048]{1,0:T(8,128)(2,1)} fusion(bf16[2048,2048]{1,0:T(8,128)(2,1)} %refs_3_.11, f32[2048,2048]{1,0:T(8,128)} %fusion.126, bf16[2048,2560]{1,0:T(8,128)(2,1)} %fusion.81.refs_8_, bf16[2048,5120]{1,0:T(8,128)(2,1)} %param.14), kind=kOutput, calls=%fused_computation.173 | convolution fusion | flops 21491613696 | bytes 54525952 | tf_op jit(solution)/shard_map/dot_general | solution.py:42
  1215.0 43.2 %collective-permute-done.11 = f32[512,2560]{1,0:T(8,128)} collective-permute-done((f32[512,2560]{1,0:T(8,128)}, f32[512,2560]{1,0:T(8,128)}, u32[]{:S(2)}, u32[]{:S(2)}) %collective-permute-start.11) | collective-permute-done | bytes 5242912 | tf_op jit(solution)/shard_map/ppermute | solution.py:146
  1409.0 36.5 %fusion.53.refs_8_ = bf16[2048,2560]{1,0:T(8,128)(2,1)} fusion(bf16[2048,2048]{1,0:T(8,128)(2,1)S(1)} %bitcast.65, bf16[2048,5120]{1,0:T(8,128)(2,1)} %get-tuple-element.179, bf16[5120,2048]{1,0:T(8,128)(2,1)} %param.13), kind=kOutput, calls=%fused_computation.111 | convolution fusion | flops 21558722560 | bytes 39845888 | tf_op jit(solution)/shard_map/dot_general | solution.py:42
  1453.2 36.8 %fusion.46.refs_9_ = bf16[2048,2560]{1,0:T(8,128)(2,1)} fusion(bf16[2048,2048]{1,0:T(8,128)(2,1)S(1)} %bitcast.59, bf16[2048,5120]{1,0:T(8,128)(2,1)} %get-tuple-element.183, bf16[5120,2048]{1,0:T(8,128)(2,1)} %param.13), kind=kOutput, calls=%fused_computation.104 | convolution fusion | flops 21558722560 | bytes 39845888 | tf_op jit(solution)/shard_map/dot_general | solution.py:42
  1532.2 38.6 %fusion.39.refs_8_ = bf16[2048,2560]{1,0:T(8,128)(2,1)} fusion(bf16[2048,2048]{1,0:T(8,128)(2,1)} %add_convert_fusion.3.refs_0_.refs_1_.refs_2_.refs_3_, bf16[2048,5120]{1,0:T(8,128)(2,1)} %get-tuple-element.179, bf16[5120,2048]{1,0:T(8,128)(2,1)} %param.13), kind=kOutput, calls=%fused_computation.97 | convolution fusion | flops 21558722560 | bytes 39845888 | tf_op jit(solution)/shard_map/dot_general | solution.py:42
  1574.1 36.4 %fusion.32.refs_9_ = bf16[2048,2560]{1,0:T(8,128)(2,1)} fusion(bf16[2048,2048]{1,0:T(8,128)(2,1)S(1)} %bitcast.61, bf16[2048,5120]{1,0:T(8,128)(2,1)} %get-tuple-element.183, bf16[5120,2048]{1,0:T(8,128)(2,1)} %param.13), kind=kOutput, calls=%fused_computation.90 | convolution fusion | flops 21558722560 | bytes 39845888 | tf_op jit(solution)/shard_map/dot_general | solution.py:42
  1685.6 136.4 %collective-permute-done.21 = f32[2560,512]{1,0:T(8,128)} collective-permute-done((f32[2560,512]{1,0:T(8,128)}, f32[2560,512]{1,0:T(8,128)}, u32[]{:S(2)}, u32[]{:S(2)}) %collective-permute-start.21) | collective-permute-done | bytes 5242912 | tf_op jit(solution)/shard_map/ppermute | solution.py:146
  2123.1 204.9 %collective-permute-done.27 = f32[512,2560]{1,0:T(8,128)S(1)} collective-permute-done((f32[512,2560]{1,0:T(8,128)}, f32[512,2560]{1,0:T(8,128)S(1)}, u32[]{:S(2)}, u32[]{:S(2)}) %collective-permute-start.27) | collective-permute-done | bytes 5242912 | tf_op jit(solution)/shard_map/ppermute | solution.py:146
  2401.6 102.7 %collective-permute-done.31 = f32[256,2560]{1,0:T(8,128)S(1)} collective-permute-done((f32[256,2560]{1,0:T(8,128)S(1)}, f32[256,2560]{1,0:T(8,128)S(1)}, u32[]{:S(2)}, u32[]{:S(2)}) %collective-permute-start.31) | collective-permute-done | bytes 2621472 | tf_op jit(solution)/shard_map/ppermute | solution.py:152
  2542.0 104.6 %all-gather.23.cloned.1.call-done = f32[2048,2560]{1,0:T(8,128)} async-done(((f32[256,2560]{1,0:T(8,128)}), f32[2048,2560]{1,0:T(8,128)}) %all-gather.23.cloned.1.call-update) | async-done | bytes 20971536 | tf_op jit(solution)/shard_map/all_gather | solution.py:157
  (208 shorter events, 1093.6 us)
Async XLA Ops:
  7.2 2063.8 %all-gather.9.cloned.1.call-start = ((), (), s32[]{:S(2)}) async-start(), calls=%async_computation | async-start | bytes 23592960 | tf_op jit(solution)/shard_map/all_gather | solution.py:157
  464.8 116.5 %collective-permute-start.3 = (f32[2560,512]{1,0:T(8,128)}, f32[2560,512]{1,0:T(8,128)}, u32[]{:S(2)}, u32[]{:S(2)}) collective-permute-start(f32[2560,512]{1,0:T(8,128)} %add.348), channel_id=1, source_target_pairs={{0,2},{2,0},{1,3},{3,1},{4,6},{6,4},{5,7},{7,5}} | collective-permute-start | bytes 15728648 | tf_op jit(solution)/shard_map/ppermute | solution.py:146
  700.1 1370.8 %all-gather.11.cloned.1.call-start = ((), (), s32[]{:S(2)}) async-start(), calls=%async_computation.1 | async-start | bytes 23592960 | tf_op jit(solution)/shard_map/all_gather | solution.py:157
  700.6 200.0 %collective-permute-start.6 = (f32[2560,512]{1,0:T(8,128)}, f32[2560,512]{1,0:T(8,128)}, u32[]{:S(2)}, u32[]{:S(2)}) collective-permute-start(f32[2560,512]{1,0:T(8,128)} %add.353), channel_id=1, source_target_pairs={{0,4},{4,0},{1,5},{5,1},{2,6},{6,2},{3,7},{7,3}} | collective-permute-start | bytes 15728648 | tf_op jit(solution)/shard_map/ppermute | solution.py:146
  700.8 245.2 %collective-permute-start.7 = (f32[512,2560]{1,0:T(8,128)}, f32[512,2560]{1,0:T(8,128)}, u32[]{:S(2)}, u32[]{:S(2)}) collective-permute-start(f32[512,2560]{1,0:T(8,128)} %get-tuple-element.154), channel_id=1, source_target_pairs={{0,1},{1,0},{2,3},{3,2},{4,5},{5,4},{6,7},{7,6}} | collective-permute-start | bytes 15728648 | tf_op jit(solution)/shard_map/ppermute | solution.py:140
  1021.7 236.6 %collective-permute-start.11 = (f32[512,2560]{1,0:T(8,128)}, f32[512,2560]{1,0:T(8,128)}, u32[]{:S(2)}, u32[]{:S(2)}) collective-permute-start(f32[512,2560]{1,0:T(8,128)} %add.371), channel_id=1, source_target_pairs={{0,2},{2,0},{1,3},{3,1},{4,6},{6,4},{5,7},{7,5}} | collective-permute-start | bytes 15728648 | tf_op jit(solution)/shard_map/ppermute | solution.py:146
  1111.3 146.9 %collective-permute-start.10 = (f32[512,2560]{1,0:T(8,128)}, f32[512,2560]{1,0:T(8,128)}, u32[]{:S(2)}, u32[]{:S(2)}) collective-permute-start(f32[512,2560]{1,0:T(8,128)} %get-tuple-element.168), channel_id=1, source_target_pairs={{0,1},{1,0},{2,3},{3,2},{4,5},{5,4},{6,7},{7,6}} | collective-permute-start | bytes 15728648 | tf_op jit(solution)/shard_map/ppermute | solution.py:140
  1111.3 1224.5 %all-gather.13.cloned.1.call-start = ((), (), s32[]{:S(2)}) async-start(), calls=%async_computation.2 | async-start | bytes 23592960 | tf_op jit(solution)/shard_map/all_gather | solution.py:157
  1119.2 273.8 %collective-permute-start.13 = (f32[512,2560]{1,0:T(8,128)}, f32[512,2560]{1,0:T(8,128)}, u32[]{:S(2)}, u32[]{:S(2)}) collective-permute-start(f32[512,2560]{1,0:T(8,128)} %add.377), channel_id=1, source_target_pairs={{0,4},{4,0},{1,5},{5,1},{2,6},{6,2},{3,7},{7,3}} | collective-permute-start | bytes 15728648 | tf_op jit(solution)/shard_map/ppermute | solution.py:146
  1214.6 178.4 %collective-permute-start.12 = (f32[512,2560]{1,0:T(8,128)}, f32[512,2560]{1,0:T(8,128)}, u32[]{:S(2)}, u32[]{:S(2)}) collective-permute-start(f32[512,2560]{1,0:T(8,128)} %get-tuple-element.175), channel_id=1, source_target_pairs={{0,1},{1,0},{2,3},{3,2},{4,5},{5,4},{6,7},{7,6}} | collective-permute-start | bytes 15728648 | tf_op jit(solution)/shard_map/ppermute | solution.py:140
  1493.5 842.3 %all-gather.15.cloned.1.call-start = ((), (), s32[]{:S(2)}) async-start(), calls=%async_computation.3 | async-start | bytes 23592960 | tf_op jit(solution)/shard_map/all_gather | solution.py:157
  1498.7 111.9 %collective-permute-start.18 = (f32[256,2560]{1,0:T(8,128)}, f32[256,2560]{1,0:T(8,128)}, u32[]{:S(2)}, u32[]{:S(2)}) collective-permute-start(f32[256,2560]{1,0:T(8,128)} %get-tuple-element.230), channel_id=1, source_target_pairs={{0,2},{2,0},{1,3},{3,1},{4,6},{6,4},{5,7},{7,5}} | collective-permute-start | bytes 7864328 | tf_op jit(solution)/shard_map/ppermute | solution.py:152
  1614.2 892.0 %all-gather.19.cloned.1.call-start = ((), (), s32[]{:S(2)}) async-start(), calls=%async_computation.5 | async-start | bytes 23592960 | tf_op jit(solution)/shard_map/all_gather | solution.py:157
  1614.2 207.8 %collective-permute-start.21 = (f32[2560,512]{1,0:T(8,128)}, f32[2560,512]{1,0:T(8,128)}, u32[]{:S(2)}, u32[]{:S(2)}) collective-permute-start(f32[2560,512]{1,0:T(8,128)} %add.386), channel_id=1, source_target_pairs={{0,2},{2,0},{1,3},{3,1},{4,6},{6,4},{5,7},{7,5}} | collective-permute-start | bytes 15728648 | tf_op jit(solution)/shard_map/ppermute | solution.py:146
  1674.5 147.5 %collective-permute-start.20 = (f32[2560,512]{1,0:T(8,128)}, f32[2560,512]{1,0:T(8,128)S(1)}, u32[]{:S(2)}, u32[]{:S(2)}) collective-permute-start(f32[2560,512]{1,0:T(8,128)} %get-tuple-element.199), channel_id=1, source_target_pairs={{0,1},{1,0},{2,3},{3,2},{4,5},{5,4},{6,7},{7,6}} | collective-permute-start | bytes 15728648 | tf_op jit(solution)/shard_map/ppermute | solution.py:140
  1674.8 221.9 %collective-permute-start.23 = (f32[2560,512]{1,0:T(8,128)}, f32[2560,512]{1,0:T(8,128)}, u32[]{:S(2)}, u32[]{:S(2)}) collective-permute-start(f32[2560,512]{1,0:T(8,128)} %add.391), channel_id=1, source_target_pairs={{0,4},{4,0},{1,5},{5,1},{2,6},{6,2},{3,7},{7,3}} | collective-permute-start | bytes 15728648 | tf_op jit(solution)/shard_map/ppermute | solution.py:146
  2001.7 504.4 %all-gather.21.cloned.1.call-start = ((), (), s32[]{:S(2)}) async-start(), calls=%async_computation.6 | async-start | bytes 23592960 | tf_op jit(solution)/shard_map/all_gather | solution.py:157
  2006.1 110.2 %collective-permute-start.25 = (f32[2560,256]{1,0:T(8,128)}, f32[2560,256]{1,0:T(8,128)}, u32[]{:S(2)}, u32[]{:S(2)}) collective-permute-start(f32[2560,256]{1,0:T(8,128)} %get-tuple-element.226), channel_id=1, source_target_pairs={{0,2},{2,0},{1,3},{3,1},{4,6},{6,4},{5,7},{7,5}} | collective-permute-start | bytes 7864328 | tf_op jit(solution)/shard_map/ppermute | solution.py:152
  2119.9 422.1 %all-gather.17.cloned.1.call-start = ((), (), s32[]{:S(2)}) async-start(), calls=%async_computation.4 | async-start | bytes 23592960 | tf_op jit(solution)/shard_map/all_gather | solution.py:157
  2120.1 207.9 %collective-permute-start.27 = (f32[512,2560]{1,0:T(8,128)}, f32[512,2560]{1,0:T(8,128)S(1)}, u32[]{:S(2)}, u32[]{:S(2)}) collective-permute-start(f32[512,2560]{1,0:T(8,128)} %add.401), channel_id=1, source_target_pairs={{0,2},{2,0},{1,3},{3,1},{4,6},{6,4},{5,7},{7,5}} | collective-permute-start | bytes 15728648 | tf_op jit(solution)/shard_map/ppermute | solution.py:146
  2122.6 205.4 %collective-permute-start.26 = (f32[512,2560]{1,0:T(8,128)}, f32[512,2560]{1,0:T(8,128)}, u32[]{:S(2)}, u32[]{:S(2)}) collective-permute-start(f32[512,2560]{1,0:T(8,128)} %get-tuple-element.214), channel_id=1, source_target_pairs={{0,1},{1,0},{2,3},{3,2},{4,5},{5,4},{6,7},{7,6}} | collective-permute-start | bytes 15728648 | tf_op jit(solution)/shard_map/ppermute | solution.py:140
  2122.6 241.8 %collective-permute-start.29 = (f32[512,2560]{1,0:T(8,128)}, f32[512,2560]{1,0:T(8,128)}, u32[]{:S(2)}, u32[]{:S(2)}) collective-permute-start(f32[512,2560]{1,0:T(8,128)} %add.407), channel_id=1, source_target_pairs={{0,4},{4,0},{1,5},{5,1},{2,6},{6,2},{3,7},{7,3}} | collective-permute-start | bytes 15728648 | tf_op jit(solution)/shard_map/ppermute | solution.py:146
  2122.6 241.8 %collective-permute-start.28 = (f32[512,2560]{1,0:T(8,128)}, f32[512,2560]{1,0:T(8,128)}, u32[]{:S(2)}, u32[]{:S(2)}) collective-permute-start(f32[512,2560]{1,0:T(8,128)} %get-tuple-element.217), channel_id=1, source_target_pairs={{0,1},{1,0},{2,3},{3,2},{4,5},{5,4},{6,7},{7,6}} | collective-permute-start | bytes 15728648 | tf_op jit(solution)/shard_map/ppermute | solution.py:140
  2396.2 250.4 %all-gather.23.cloned.1.call-start = ((), (), s32[]{:S(2)}) async-start(), calls=%async_computation.7 | async-start | bytes 23592960 | tf_op jit(solution)/shard_map/all_gather | solution.py:157
  (43 other events, 2158.1 us)
Sparse Core Ops, SparseCore 0:
  700.2 190.5 all-gather.8
  1111.5 190.2 all-gather.10
  1493.6 175.8 all-gather.12
  1671.2 189.1 all-gather.14
  2001.9 179.5 all-gather.18
  2183.1 167.0 all-gather.20
  2396.3 145.6 all-gather.16
  2544.4 102.1 all-gather.22

commit v2 on v1

--- a/solution.py
+++ b/solution.py
@@ -14,11 +14,11 @@
 STEPS = (
     ("F1", 0), ("F1", 1), ("F2", 0), ("F2", 1),
     ("F3", 0, 0), ("F3", 0, 1), ("S", 4, 0), ("F3", 1, 0), ("C", 4, 0), ("F3", 1, 1), ("S", 4, 1), ("K", 4, 0), ("C", 4, 1), ("K", 4, 1),
-    ("U", 4, 0), ("B3", 0, 0), ("B3", 0, 1), ("S", 3, 0), ("G", 4, 0), ("U", 4, 1), ("B3", 1, 0), ("C", 3, 0), ("B3", 1, 1), ("S", 3, 1), ("G", 4, 1),
-    ("K", 3, 0), ("C", 3, 1), ("K", 3, 1), ("B2", 0), ("U", 3, 0), ("B2", 1), ("S", 2, 0), ("S", 2, 1), ("U", 3, 1), ("C", 2, 0), ("B1", 0, 0),
-    ("C", 2, 1), ("B1", 0, 1), ("G", 3, 0), ("S", 1, 0), ("B1", 1, 0), ("C", 1, 0), ("B1", 1, 1), ("G", 3, 1), ("S", 1, 1), ("K", 2, 0), ("C", 1, 1), ("U", 2, 0),
-    ("K", 2, 1), ("K", 1, 0), ("U", 2, 1), ("K", 1, 1), ("BX", 0), ("G", 2, 0), ("BX", 1), ("R", 4), ("G", 2, 1), ("U", 1, 0), ("R", 3),
-    ("U", 1, 1), ("G", 1, 0), ("G", 1, 1), ("R", 2), ("R", 1),
+    ("U", 4, 0), ("B3", 0, 0), ("B3", 0, 1), ("U", 4, 1), ("S", 3, 0), ("B3", 1, 0), ("C", 3, 0), ("G", 4, 0), ("B3", 1, 1), ("G", 4, 1), ("S", 3, 1),
+    ("K", 3, 0), ("C", 3, 1), ("K", 3, 1), ("B2", 0), ("B2", 1), ("U", 3, 0), ("S", 2, 0), ("S", 2, 1), ("C", 2, 0), ("B1", 0, 0), ("G", 3, 0),
+    ("C", 2, 1), ("U", 3, 1), ("B1", 0, 1), ("S", 1, 0), ("K", 2, 0), ("C", 1, 0), ("G", 3, 1), ("B1", 1, 0), ("U", 2, 0), ("B1", 1, 1), ("S", 1, 1), ("K", 2, 1), ("C", 1, 1),
+    ("U", 2, 1), ("K", 1, 0), ("G", 2, 0), ("K", 1, 1), ("BX", 0), ("G", 2, 1), ("U", 1, 0), ("BX", 1), ("U", 1, 1), ("R", 4),
+    ("G", 1, 0), ("R", 3), ("G", 1, 1), ("R", 2), ("Q", 1), ("R", 1),
 )
 
 
@@ -127,6 +127,7 @@
             def __init__(self, dim_ops, wide_first):
                 self.dim_ops, self.wide_first = dim_ops, wide_first
                 self.axis = 1 if wide_first else 0
+                self.base = None
                 self.ff_ops, self.send, self.keep, self.chip, self.rows, self.full = {}, {}, {}, {}, {}, {}
 
             def link(self, color, second):
@@ -156,7 +157,14 @@
                 shard = mark(at(kept) + got)
                 self.full[color] = lax.all_gather(shard, ("dx", "dz", "dy"), axis=self.axis, tiled=True)
 
+            def begin(self):
+                pads = [(0, 0), (0, 0)]
+                pads[1 - self.axis] = (0, half_ff)
+                self.base = mark(jnp.pad(at(self.full[0]) / dev_count, pads))
+
             def result(self):
+                if self.base is not None:
+                    return mark(lax.dynamic_update_slice_in_dim(at(self.base), self.full[1] / dev_count, half_ff, axis=1 - self.axis))
                 parts = [at(self.full[0]), self.full[1]]
                 return mark(jnp.concatenate(parts, axis=1 - self.axis) / dev_count)
 
@@ -218,6 +226,8 @@
                 grads[args[0]].add_rows(args[1])
             elif name == "G":
                 grads[args[0]].gather(args[1])
+            elif name == "Q":
+                grads[args[0]].begin()
             else:
                 results[args[0]] = grads[args[0]].result()
         return results[1], results[2], results[3], results[4], dx_rows[0], dx_rows[1]

time: 2690 us -> 2620 us (0.974)
  waiting for transfers between devices: 965 us -> 872 us
    ppermute x8, waiting for transfers between devices: 652 us -> 595 us  [add_chip(): self.chip[color] = lax.ppermute(chip, self.link(color, False), SWAP)]
    div x4 -> x3, other arithmetic: 117 us -> 86.5 us  [result(): return mark(jnp.concatenate(parts, axis=1 - self.axis) / dev_count)]
    all_gather x8, waiting for transfers between devices: 111 us -> 84.2 us  [gather(): lax.all_gather(shard, ('dx', 'dz', 'dy'), axis=self.axis, tiled=True)]
  transfers between devices with their start and end apart: 40 -> 40, of which waited for: 12 -> 14; matrix products, arithmetic and copies ran while one was open for 29% -> 33% of each run, Pallas kernels for 15% -> 16%
where the time goes in v2:
time: 2620 us; the launch traced here: 2610 us
  matrix products  910 us (35%)
  waiting for transfers between devices  872 us (33%)
  Pallas kernels  474 us (18%)
  other arithmetic  259 us (10%)
  local copies, waits for them, and re-layouts  47.1 us (2%)
  starting transfers between devices  30.2 us (1%)
    ppermute x8, waiting for transfers between devices, add_chip(): self.chip[color] = lax.ppermute(chip, self.link(color, False), SWAP)  595 us
    dot_general x16, matrix products, mat_nt(): lax.dot_general(left_op, right_op, (((1,), (1,)), ((), ())), preferred_el...  552 us
    pallas_call x16, Pallas kernels, grad_blocks(): pl.pallas_call(body, grid_spec=pltpu.PrefetchScalarGridSpec(num_scalar_pr...  474 us
    dot_general x8, matrix products, mat_nn(): return jnp.dot(left_op, right_op, preferred_element_type=jnp.float32)  358 us
    ppermute x8, waiting for transfers between devices, add_rows(): self.rows[color] = (kept, lax.ppermute(out, self.link(color, True), SWAP))  185 us
    div x3, other arithmetic, result(): return mark(jnp.concatenate(parts, axis=1 - self.axis) / dev_count)  86.5 us
    all_gather x8, waiting for transfers between devices, gather(): lax.all_gather(shard, ('dx', 'dz', 'dy'), axis=self.axis, tiled=True)  84.2 us
    add x8, other arithmetic, add_rows(): total = mark(at(own) + got + self.chip[color])  63.1 us
  transfers between devices with their start and end apart: 40, of which 14 were waited for; matrix products, arithmetic and copies ran while one was open for 33% of the time, Pallas kernels for 16%

profile of v2, /device:TPU:0, one launch (start us, length us, event | category | flops | bytes accessed | tf_op | source)
XLA Modules:
  0.0 2607.5 jit_solution(12749765916852652307)
XLA Ops:
  7.2 61.9 %fusion.1 = (bf16[2048,5120]{1,0:T(8,128)(2,1)}, bf16[2048,5120]{1,0:T(8,128)(2,1)}) fusion(bf16[2048,2048]{1,0:T(8,128)(2,1)} %refs_3_.15, bf16[2048,5120]{1,0:T(8,128)(2,1)} %param.12), kind=kOutput, calls=%fused_computation.11 | convolution fusion | flops 43065016320 | bytes 71303168 | tf_op jit(solution)/shard_map/dot_general | solution.py:38
  69.1 60.2 %fusion.6 = (bf16[2048,5120]{1,0:T(8,128)(2,1)}, bf16[2048,5120]{1,0:T(8,128)(2,1)}) fusion(bf16[2048,2048]{1,0:T(8,128)(2,1)S(1)} %copy-done, bf16[2048,5120]{1,0:T(8,128)(2,1)} %param.12), kind=kOutput, calls=%fused_computation.16 | convolution fusion | flops 43065016320 | bytes 71303168 | tf_op jit(solution)/shard_map/dot_general | solution.py:38
  129.3 53.2 %add_convert_fusion.5.refs_0_.refs_1_.refs_2_.refs_3_ = bf16[2048,2048]{1,0:T(8,128)(2,1)} fusion(bf16[2048,2048]{1,0:T(8,128)(2,1)} %refs_3_.15, bf16[2048,5120]{1,0:T(8,128)(2,1)} %get-tuple-element.198.refs_8_, bf16[5120,2048]{1,0:T(8,128)(2,1)} %param.13), kind=kOutput, calls=%fused_computation.175 | convolution fusion | flops 42962255872 | bytes 58720256 | tf_op jit(solution)/shard_map/dot_general | solution.py:38
  182.5 52.9 %add_convert_fusion.4.refs_4_.refs_5_.refs_6_.refs_7_ = bf16[2048,2048]{1,0:T(8,128)(2,1)} fusion(bf16[2048,2048]{1,0:T(8,128)(2,1)} %refs_7_.15, bf16[2048,5120]{1,0:T(8,128)(2,1)} %get-tuple-element.117.refs_9_, bf16[5120,2048]{1,0:T(8,128)(2,1)} %param.13), kind=kOutput, calls=%fused_computation.174 | convolution fusion | flops 42962255872 | bytes 58720256 | tf_op jit(solution)/shard_map/dot_general | solution.py:38
  235.4 32.9 %fusion.91 = (bf16[2048,2560]{1,0:T(8,128)(2,1)}, bf16[2048,2560]{1,0:T(8,128)(2,1)}) fusion(bf16[2048,2048]{1,0:T(8,128)(2,1)} %add_convert_fusion.5.refs_0_.refs_1_.refs_2_.refs_3_, bf16[2048,5120]{1,0:T(8,128)(2,1)} %param.14), kind=kOutput, calls=%fused_computation.148 | convolution fusion | flops 21532508160 | bytes 39845888 | tf_op jit(solution)/shard_map/dot_general | solution.py:38
  268.3 31.9 %fusion.96 = (bf16[2048,2560]{1,0:T(8,128)(2,1)}, bf16[2048,2560]{1,0:T(8,128)(2,1)}) fusion(bf16[2048,2048]{1,0:T(8,128)(2,1)S(1)} %copy-done.1, bf16[2048,5120]{1,0:T(8,128)(2,1)} %param.14), kind=kOutput, calls=%fused_computation.153 | convolution fusion | flops 21532508160 | bytes 39845888 | tf_op jit(solution)/shard_map/dot_general | solution.py:38
  331.3 33.2 %fusion.101 = (bf16[2048,2560]{1,0:T(8,128)(2,1)}, bf16[2048,2560]{1,0:T(8,128)(2,1)}) fusion(bf16[2048,2048]{1,0:T(8,128)(2,1)} %add_convert_fusion.5.refs_0_.refs_1_.refs_2_.refs_3_, bf16[2048,5120]{1,0:T(8,128)(2,1)} %param.14), kind=kOutput, calls=%fused_computation.158 | convolution fusion | flops 21532508160 | bytes 39845888 | tf_op jit(solution)/shard_map/dot_general | solution.py:38
  504.7 44.5 %collective-permute-done.3 = f32[2560,512]{1,0:T(8,128)} collective-permute-done((f32[2560,512]{1,0:T(8,128)}, f32[2560,512]{1,0:T(8,128)}, u32[]{:S(2)}, u32[]{:S(2)}) %collective-permute-start.3) | collective-permute-done | bytes 5242912 | tf_op jit(solution)/shard_map/ppermute | solution.py:147
  556.7 36.1 %fusion.81.refs_8_ = bf16[2048,2560]{1,0:T(8,128)(2,1)} fusion(bf16[2048,2560]{1,0:T(8,128)(2,1)} %get-tuple-element.143, bf16[2048,2048]{1,0:T(8,128)(2,1)S(1)} %bitcast.53, bf16[5120,2048]{1,0:T(8,128)(2,1)} %param.15), kind=kOutput, calls=%fused_computation.138 | convolution fusion | flops 21558722560 | bytes 39845888 | tf_op jit(solution)/shard_map/dot_general | solution.py:42
  592.8 37.4 %fusion.74.refs_9_ = bf16[2048,2560]{1,0:T(8,128)(2,1)} fusion(bf16[2048,2560]{1,0:T(8,128)(2,1)} %get-tuple-element.145, bf16[2048,2048]{1,0:T(8,128)(2,1)} %refs_7_.11, bf16[5120,2048]{1,0:T(8,128)(2,1)} %param.15), kind=kOutput, calls=%fused_computation.131 | convolution fusion | flops 21558722560 | bytes 39845888 | tf_op jit(solution)/shard_map/dot_general | solution.py:42
  672.7 36.9 %fusion.67.refs_8_ = bf16[2048,2560]{1,0:T(8,128)(2,1)} fusion(bf16[2048,2560]{1,0:T(8,128)(2,1)} %get-tuple-element.151, bf16[2048,2048]{1,0:T(8,128)(2,1)} %refs_3_.11, bf16[5120,2048]{1,0:T(8,128)(2,1)} %param.15), kind=kOutput, calls=%fused_computation.124 | convolution fusion | flops 21558722560 | bytes 39845888 | tf_op jit(solution)/shard_map/dot_general | solution.py:42
  720.8 38.4 %fusion.60.refs_9_ = bf16[2048,2560]{1,0:T(8,128)(2,1)} fusion(bf16[2048,2560]{1,0:T(8,128)(2,1)} %get-tuple-element.156, bf16[2048,2048]{1,0:T(8,128)(2,1)} %refs_7_.11, bf16[5120,2048]{1,0:T(8,128)(2,1)} %param.15), kind=kOutput, calls=%fused_computation.117 | convolution fusion | flops 21558722560 | bytes 39845888 | tf_op jit(solution)/shard_map/dot_general | solution.py:42
  759.2 67.4 %collective-permute-done.8 = f32[2560,256]{1,0:T(8,128)S(1)} collective-permute-done((f32[2560,256]{1,0:T(8,128)S(1)}, f32[2560,256]{1,0:T(8,128)S(1)}, u32[]{:S(2)}, u32[]{:S(2)}) %collective-permute-start.8) | collective-permute-done | bytes 2621472 | tf_op jit(solution)/shard_map/ppermute | solution.py:153
  957.2 32.5 %add_convert_fusion.3.refs_0_.refs_1_.refs_2_.refs_3_ = bf16[2048,2048]{1,0:T(8,128)(2,1)} fusion(bf16[2048,2048]{1,0:T(8,128)(2,1)} %refs_3_.11, f32[2048,2048]{1,0:T(8,128)} %fusion.126, bf16[2048,2560]{1,0:T(8,128)(2,1)} %fusion.81.refs_8_, bf16[2048,5120]{1,0:T(8,128)(2,1)} %param.14), kind=kOutput, calls=%fused_computation.173 | convolution fusion | flops 21491613696 | bytes 54525952 | tf_op jit(solution)/shard_map/dot_general | solution.py:42
  1141.9 38.8 %fusion.53.refs_8_ = bf16[2048,2560]{1,0:T(8,128)(2,1)} fusion(bf16[2048,2048]{1,0:T(8,128)(2,1)} %add_convert_fusion.3.refs_0_.refs_1_.refs_2_.refs_3_, bf16[2048,5120]{1,0:T(8,128)(2,1)} %get-tuple-element.177, bf16[5120,2048]{1,0:T(8,128)(2,1)} %param.13), kind=kOutput, calls=%fused_computation.110 | convolution fusion | flops 21558722560 | bytes 39845888 | tf_op jit(solution)/shard_map/dot_general | solution.py:42
  1200.7 183.7 %collective-permute-done.16 = f32[512,2560]{1,0:T(8,128)S(1)} collective-permute-done((f32[512,2560]{1,0:T(8,128)}, f32[512,2560]{1,0:T(8,128)S(1)}, u32[]{:S(2)}, u32[]{:S(2)}) %collective-permute-start.16) | collective-permute-done | bytes 5242912 | tf_op jit(solution)/shard_map/ppermute | solution.py:147
  1390.8 38.7 %fusion.46.refs_9_ = bf16[2048,2560]{1,0:T(8,128)(2,1)} fusion(bf16[2048,2048]{1,0:T(8,128)(2,1)} %add_convert_fusion.2.refs_4_.refs_5_.refs_6_.refs_7_, bf16[2048,5120]{1,0:T(8,128)(2,1)} %get-tuple-element.184, bf16[5120,2048]{1,0:T(8,128)(2,1)} %param.13), kind=kOutput, calls=%fused_computation.103 | convolution fusion | flops 21558722560 | bytes 39845888 | tf_op jit(solution)/shard_map/dot_general | solution.py:42
  1531.2 41.5 %fusion.39.refs_8_ = bf16[2048,2560]{1,0:T(8,128)(2,1)} fusion(bf16[2048,2048]{1,0:T(8,128)(2,1)} %add_convert_fusion.3.refs_0_.refs_1_.refs_2_.refs_3_, bf16[2048,5120]{1,0:T(8,128)(2,1)} %get-tuple-element.177, bf16[5120,2048]{1,0:T(8,128)(2,1)} %param.13), kind=kOutput, calls=%fused_computation.96 | convolution fusion | flops 21558722560 | bytes 39845888 | tf_op jit(solution)/shard_map/dot_general | solution.py:42
  1572.7 154.6 %collective-permute-done.20 = f32[2560,512]{1,0:T(8,128)} collective-permute-done((f32[2560,512]{1,0:T(8,128)}, f32[2560,512]{1,0:T(8,128)}, u32[]{:S(2)}, u32[]{:S(2)}) %collective-permute-start.20) | collective-permute-done | bytes 5242912 | tf_op jit(solution)/shard_map/ppermute | solution.py:147
  1735.7 36.2 %fusion.32.refs_9_ = bf16[2048,2560]{1,0:T(8,128)(2,1)} fusion(bf16[2048,2048]{1,0:T(8,128)(2,1)S(1)} %bitcast.57, bf16[2048,5120]{1,0:T(8,128)(2,1)} %get-tuple-element.184, bf16[5120,2048]{1,0:T(8,128)(2,1)} %param.13), kind=kOutput, calls=%fused_computation.89 | convolution fusion | flops 21558722560 | bytes 39845888 | tf_op jit(solution)/shard_map/dot_general | solution.py:42
  1967.2 35.1 %add_convert_fusion.1 = bf16[2048,2048]{1,0:T(8,128)(2,1)} fusion(bf16[2048,2048]{1,0:T(8,128)(2,1)} %add_convert_fusion.3.refs_0_.refs_1_.refs_2_.refs_3_, f32[2048,2048]{1,0:T(8,128)} %fusion.114, bf16[2048,2560]{1,0:T(8,128)(2,1)} %fusion.53.refs_8_, bf16[2048,5120]{1,0:T(8,128)(2,1)} %param.12), kind=kOutput, calls=%fused_computation.171 | convolution fusion | flops 21491613696 | bytes 54525952 | tf_op jit(solution)/shard_map/dot_general | solution.py:42
  2021.9 202.6 %collective-permute-done.27 = f32[512,2560]{1,0:T(8,128)S(1)} collective-permute-done((f32[512,2560]{1,0:T(8,128)}, f32[512,2560]{1,0:T(8,128)S(1)}, u32[]{:S(2)}, u32[]{:S(2)}) %collective-permute-start.27) | collective-permute-done | bytes 5242912 | tf_op jit(solution)/shard_map/ppermute | solution.py:147
  2372.3 71.2 %collective-permute-done.31 = f32[256,2560]{1,0:T(8,128)} collective-permute-done((f32[256,2560]{1,0:T(8,128)}, f32[256,2560]{1,0:T(8,128)}, u32[]{:S(2)}, u32[]{:S(2)}) %collective-permute-start.31) | collective-permute-done | bytes 2621472 | tf_op jit(solution)/shard_map/ppermute | solution.py:153
  2503.4 80.6 %all-gather.23.cloned.1.call-done = f32[2048,2560]{1,0:T(8,128)} async-done(((f32[256,2560]{1,0:T(8,128)}), f32[2048,2560]{1,0:T(8,128)}) %all-gather.23.cloned.1.call-update) | async-done | bytes 20971536 | tf_op jit(solution)/shard_map/all_gather | solution.py:158
  (199 shorter events, 1090.4 us)
Async XLA Ops:
  7.2 2297.6 %all-gather.9.cloned.1.call-start = ((), (), s32[]{:S(2)}) async-start(), calls=%async_computation | async-start | bytes 23592960 | tf_op jit(solution)/shard_map/all_gather | solution.py:158
  432.7 116.5 %collective-permute-start.3 = (f32[2560,512]{1,0:T(8,128)}, f32[2560,512]{1,0:T(8,128)}, u32[]{:S(2)}, u32[]{:S(2)}) collective-permute-start(f32[2560,512]{1,0:T(8,128)} %add.350), channel_id=1, source_target_pairs={{0,2},{2,0},{1,3},{3,1},{4,6},{6,4},{5,7},{7,5}} | collective-permute-start | bytes 15728648 | tf_op jit(solution)/shard_map/ppermute | solution.py:147
  473.5 161.2 %collective-permute-start.5 = (f32[2560,512]{1,0:T(8,128)}, f32[2560,512]{1,0:T(8,128)}, u32[]{:S(2)}, u32[]{:S(2)}) collective-permute-start(f32[2560,512]{1,0:T(8,128)} %add.355), channel_id=1, source_target_pairs={{0,4},{4,0},{1,5},{5,1},{2,6},{6,2},{3,7},{7,3}} | collective-permute-start | bytes 15728648 | tf_op jit(solution)/shard_map/ppermute | solution.py:147
  716.4 1588.4 %all-gather.11.cloned.1.call-start = ((), (), s32[]{:S(2)}) async-start(), calls=%async_computation.1 | async-start | bytes 23592960 | tf_op jit(solution)/shard_map/all_gather | solution.py:158
  719.3 107.4 %collective-permute-start.8 = (f32[2560,256]{1,0:T(8,128)S(1)}, f32[2560,256]{1,0:T(8,128)S(1)}, u32[]{:S(2)}, u32[]{:S(2)}) collective-permute-start(f32[2560,256]{1,0:T(8,128)S(1)} %get-tuple-element.234), channel_id=1, source_target_pairs={{0,2},{2,0},{1,3},{3,1},{4,6},{6,4},{5,7},{7,5}} | collective-permute-start | bytes 7864328 | tf_op jit(solution)/shard_map/ppermute | solution.py:153
  857.9 201.8 %collective-permute-start.11 = (f32[512,2560]{1,0:T(8,128)}, f32[512,2560]{1,0:T(8,128)}, u32[]{:S(2)}, u32[]{:S(2)}) collective-permute-start(f32[512,2560]{1,0:T(8,128)} %add.372), channel_id=1, source_target_pairs={{0,2},{2,0},{1,3},{3,1},{4,6},{6,4},{5,7},{7,5}} | collective-permute-start | bytes 15728648 | tf_op jit(solution)/shard_map/ppermute | solution.py:147
  860.4 1483.1 %all-gather.17.cloned.1.call-start = ((), (), s32[]{:S(2)}) async-start(), calls=%async_computation.4 | async-start | bytes 23592960 | tf_op jit(solution)/shard_map/all_gather | solution.py:158
  890.6 169.1 %collective-permute-start.10 = (f32[512,2560]{1,0:T(8,128)}, f32[512,2560]{1,0:T(8,128)}, u32[]{:S(2)}, u32[]{:S(2)}) collective-permute-start(f32[512,2560]{1,0:T(8,128)} %get-tuple-element.169), channel_id=1, source_target_pairs={{0,1},{1,0},{2,3},{3,2},{4,5},{5,4},{6,7},{7,6}} | collective-permute-start | bytes 15728648 | tf_op jit(solution)/shard_map/ppermute | solution.py:141
  1184.3 1159.2 %all-gather.19.cloned.1.call-start = ((), (), s32[]{:S(2)}) async-start(), calls=%async_computation.5 | async-start | bytes 23592960 | tf_op jit(solution)/shard_map/all_gather | solution.py:158
  1184.9 199.6 %collective-permute-start.16 = (f32[512,2560]{1,0:T(8,128)}, f32[512,2560]{1,0:T(8,128)S(1)}, u32[]{:S(2)}, u32[]{:S(2)}) collective-permute-start(f32[512,2560]{1,0:T(8,128)} %add.379), channel_id=1, source_target_pairs={{0,4},{4,0},{1,5},{5,1},{2,6},{6,2},{3,7},{7,3}} | collective-permute-start | bytes 15728648 | tf_op jit(solution)/shard_map/ppermute | solution.py:147
  1528.0 919.1 %all-gather.15.cloned.1.call-start = ((), (), s32[]{:S(2)}) async-start(), calls=%async_computation.3 | async-start | bytes 23592960 | tf_op jit(solution)/shard_map/all_gather | solution.py:158
  1528.1 199.2 %collective-permute-start.20 = (f32[2560,512]{1,0:T(8,128)}, f32[2560,512]{1,0:T(8,128)}, u32[]{:S(2)}, u32[]{:S(2)}) collective-permute-start(f32[2560,512]{1,0:T(8,128)} %add.386), channel_id=1, source_target_pairs={{0,2},{2,0},{1,3},{3,1},{4,6},{6,4},{5,7},{7,5}} | collective-permute-start | bytes 15728648 | tf_op jit(solution)/shard_map/ppermute | solution.py:147
  1529.8 316.4 %collective-permute-start.23 = (f32[2560,512]{1,0:T(8,128)}, f32[2560,512]{1,0:T(8,128)}, u32[]{:S(2)}, u32[]{:S(2)}) collective-permute-start(f32[2560,512]{1,0:T(8,128)} %add.392), channel_id=1, source_target_pairs={{0,4},{4,0},{1,5},{5,1},{2,6},{6,2},{3,7},{7,3}} | collective-permute-start | bytes 15728648 | tf_op jit(solution)/shard_map/ppermute | solution.py:147
  1531.2 196.1 %collective-permute-start.19 = (f32[2560,512]{1,0:T(8,128)}, f32[2560,512]{1,0:T(8,128)}, u32[]{:S(2)}, u32[]{:S(2)}) collective-permute-start(f32[2560,512]{1,0:T(8,128)} %get-tuple-element.194), channel_id=1, source_target_pairs={{0,1},{1,0},{2,3},{3,2},{4,5},{5,4},{6,7},{7,6}} | collective-permute-start | bytes 15728648 | tf_op jit(solution)/shard_map/ppermute | solution.py:141
  1900.6 546.6 %all-gather.21.cloned.1.call-start = ((), (), s32[]{:S(2)}) async-start(), calls=%async_computation.6 | async-start | bytes 23592960 | tf_op jit(solution)/shard_map/all_gather | solution.py:158
  1906.0 108.3 %collective-permute-start.25 = (f32[2560,256]{1,0:T(8,128)}, f32[2560,256]{1,0:T(8,128)}, u32[]{:S(2)}, u32[]{:S(2)}) collective-permute-start(f32[2560,256]{1,0:T(8,128)} %get-tuple-element.226), channel_id=1, source_target_pairs={{0,2},{2,0},{1,3},{3,1},{4,6},{6,4},{5,7},{7,5}} | collective-permute-start | bytes 7864328 | tf_op jit(solution)/shard_map/ppermute | solution.py:153
  2018.0 462.0 %all-gather.13.cloned.1.call-start = ((), (), s32[]{:S(2)}) async-start(), calls=%async_computation.2 | async-start | bytes 23592960 | tf_op jit(solution)/shard_map/all_gather | solution.py:158
  2018.0 206.5 %collective-permute-start.27 = (f32[512,2560]{1,0:T(8,128)}, f32[512,2560]{1,0:T(8,128)S(1)}, u32[]{:S(2)}, u32[]{:S(2)}) collective-permute-start(f32[512,2560]{1,0:T(8,128)} %add.399), channel_id=1, source_target_pairs={{0,2},{2,0},{1,3},{3,1},{4,6},{6,4},{5,7},{7,5}} | collective-permute-start | bytes 15728648 | tf_op jit(solution)/shard_map/ppermute | solution.py:147
  2020.5 204.0 %collective-permute-start.26 = (f32[512,2560]{1,0:T(8,128)}, f32[512,2560]{1,0:T(8,128)}, u32[]{:S(2)}, u32[]{:S(2)}) collective-permute-start(f32[512,2560]{1,0:T(8,128)} %get-tuple-element.212), channel_id=1, source_target_pairs={{0,1},{1,0},{2,3},{3,2},{4,5},{5,4},{6,7},{7,6}} | collective-permute-start | bytes 15728648 | tf_op jit(solution)/shard_map/ppermute | solution.py:141
  2020.5 274.7 %collective-permute-start.29 = (f32[512,2560]{1,0:T(8,128)}, f32[512,2560]{1,0:T(8,128)}, u32[]{:S(2)}, u32[]{:S(2)}) collective-permute-start(f32[512,2560]{1,0:T(8,128)} %add.411), channel_id=1, source_target_pairs={{0,4},{4,0},{1,5},{5,1},{2,6},{6,2},{3,7},{7,3}} | collective-permute-start | bytes 15728648 | tf_op jit(solution)/shard_map/ppermute | solution.py:147
  2021.7 273.5 %collective-permute-start.28 = (f32[512,2560]{1,0:T(8,128)}, f32[512,2560]{1,0:T(8,128)}, u32[]{:S(2)}, u32[]{:S(2)}) collective-permute-start(f32[512,2560]{1,0:T(8,128)} %get-tuple-element.215), channel_id=1, source_target_pairs={{0,1},{1,0},{2,3},{3,2},{4,5},{5,4},{6,7},{7,6}} | collective-permute-start | bytes 15728648 | tf_op jit(solution)/shard_map/ppermute | solution.py:141
  2232.9 100.3 %collective-permute-start.30 = (f32[256,2560]{1,0:T(8,128)}, f32[256,2560]{1,0:T(8,128)}, u32[]{:S(2)}, u32[]{:S(2)}) collective-permute-start(f32[256,2560]{1,0:T(8,128)} %get-tuple-element.224), channel_id=1, source_target_pairs={{0,4},{4,0},{1,5},{5,1},{2,6},{6,2},{3,7},{7,3}} | collective-permute-start | bytes 7864328 | tf_op jit(solution)/shard_map/ppermute | solution.py:153
  2337.0 247.0 %all-gather.23.cloned.1.call-start = ((), (), s32[]{:S(2)}) async-start(), calls=%async_computation.7 | async-start | bytes 23592960 | tf_op jit(solution)/shard_map/all_gather | solution.py:158
  2341.4 102.1 %collective-permute-start.31 = (f32[256,2560]{1,0:T(8,128)}, f32[256,2560]{1,0:T(8,128)}, u32[]{:S(2)}, u32[]{:S(2)}) collective-permute-start(f32[256,2560]{1,0:T(8,128)} %get-tuple-element.222), channel_id=1, source_target_pairs={{0,2},{2,0},{1,3},{3,1},{4,6},{6,4},{5,7},{7,5}} | collective-permute-start | bytes 7864328 | tf_op jit(solution)/shard_map/ppermute | solution.py:153
  (39 other events, 2223.5 us)
Sparse Core Ops, SparseCore 0:
  716.5 152.1 all-gather.8
  870.5 186.3 all-gather.10
  1184.4 187.3 all-gather.16
  1528.2 187.3 all-gather.18
  1900.7 180.9 all-gather.14
  2083.4 164.7 all-gather.20
  2337.1 142.8 all-gather.12
  2481.8 102.1 all-gather.22
